TPU v7x, 32 devices: a whole 2x2x4 slice. The times are simulated.
32 devices in a mesh: gz: 16 (over z, y, core), gy: 2 (over x).
Axes of the slice: x: 2, y: 2, z: 4, core: 2. Of those that a mesh axis runs over, the one named last changes fastest.
Arguments:
- fixed_image: float32 [160, 80, 320], P('gz', 'gy'), may hold values from -6 to 6
- moving_image: float32 [160, 80, 320], P('gz', 'gy'), may hold values from -6 to 6
- moving_grad: float32 [3, 160, 80, 320], P(None, 'gz', 'gy'), may hold values from -6 to 6
Outputs:
- control_grad: float32 [32, 3, 16, 64], P('gz', None, 'gy')
All inputs are finite; a program needn't handle non-finite values.
Results may differ from a plain program's by a relative error of at most 0.00016.
Values sent between devices are 32-bit elements; how exact they have to be, the bound alone decides.
A program may use at most 64 MiB of HBM per device.

v0:
```python
import jax
import jax.numpy as jnp
from jax import lax
from jax.sharding import PartitionSpec as P

RADIUS = 4
SPACING = 5


EPS = 36.0
SIM_WEIGHT = 8.0


def passed_along(block, axis, distance):
    devices = range(lax.axis_size(axis))
    route = [(i - distance, i) for i in devices if i - distance in devices]
    return lax.ppermute(block, axis, route)


def padded(shard, sides, width):
    for axis, dim in sides:
        count, length = (lax.axis_size(axis), shard.shape[dim])
        up = [(i, (i + 1) % count) for i in range(count - 1)]
        down = [(j, i) for i, j in up]
        last = lax.slice_in_dim(shard, length - width, length, axis=dim)
        leading = lax.slice_in_dim(shard, 0, width, axis=dim)
        before = lax.ppermute(last, axis, up)
        after = lax.ppermute(leading, axis, down)
        shard = jnp.concatenate([before, shard, after], axis=dim)
    return shard


def spline_basis(voxels, points, anchor, first_point, columns):
    position = anchor + jnp.arange(voxels, dtype=jnp.int32)
    cell_index = position // SPACING
    fraction = (position - cell_index * SPACING).astype(jnp.float32) / SPACING
    remainder = 1.0 - fraction
    weights = [
        remainder**3 / 6.0,
        (3.0 * fraction**3 - 6.0 * fraction**2 + 4.0) / 6.0,
        (-3.0 * fraction**3 + 3.0 * fraction**2 + 3.0 * fraction + 1.0) / 6.0,
        fraction**3 / 6.0,
    ]
    targets = first_point + jnp.arange(columns, dtype=jnp.int32)
    matrix = jnp.zeros((voxels, columns), jnp.float32)
    for spline in range(4):
        clamped = jnp.clip(cell_index - 1 + spline, 0, points - 1)
        matrix = matrix + weights[spline][:, None] * (clamped[:, None] == targets[None, :]).astype(
            jnp.float32
        )
    return matrix


def box_along(values, dimension, length):
    running = lax.slice_in_dim(values, 0, length, axis=dimension)
    for offset in range(1, 2 * RADIUS + 1):
        running = running + lax.slice_in_dim(values, offset, offset + length, axis=dimension)
    return running


def box_three(values, plane_count, height):
    last_dim = values.ndim - 1
    widths = [(0, 0)] * last_dim + [(RADIUS, RADIUS)]
    summed = box_along(jnp.pad(values, widths), last_dim, values.shape[last_dim])
    summed = box_along(summed, last_dim - 1, height)
    return box_along(summed, last_dim - 2, plane_count)


def coefficient_fields(images):
    plane_count = images.shape[1] - 2 * RADIUS
    height = images.shape[2] - 2 * RADIUS
    fixed_part = images[0]
    moving_part = images[1]
    window_size = float((2 * RADIUS + 1) ** 3)
    sum_f = box_three(fixed_part, plane_count, height)
    sum_m = box_three(moving_part, plane_count, height)
    sum_ff = box_three(fixed_part * fixed_part, plane_count, height)
    sum_mm = box_three(moving_part * moving_part, plane_count, height)
    sum_fm = box_three(fixed_part * moving_part, plane_count, height)
    covariance = sum_fm - sum_f * sum_m / window_size
    variance_fixed = sum_ff - sum_f * sum_f / window_size + EPS
    variance_moving = sum_mm - sum_m * sum_m / window_size + EPS
    quotient = covariance / (variance_fixed * variance_moving)
    weight_cross = 2.0 * quotient
    weight_moving = -quotient * covariance / variance_moving
    return jnp.stack(
        [
            weight_cross,
            weight_cross * sum_f / window_size,
            weight_moving,
            weight_moving * sum_m / window_size,
        ]
    )


def from_neighbour(outgoing, offset):
    return passed_along(outgoing, "gz", offset)


def row_sum(partial_sums):
    return lax.psum_scatter(partial_sums, "gy", scatter_dimension=2, tiled=True)


def combine_slabs(partial_sums, owned_points):
    result = partial_sums[1 : owned_points + 1]
    offsets = [-1, 1] + []
    for offset in offsets:
        if offset < 0:
            outgoing = partial_sums[0:1]
            target = owned_points - 1
        else:
            first_row = 1 + offset * owned_points
            last_row = min(owned_points + offset * owned_points, owned_points + 2)
            outgoing = partial_sums[first_row : last_row + 1]
            target = first_row - offset * owned_points - 1
        arrived = from_neighbour(outgoing, offset)
        result = result.at[target : target + arrived.shape[0]].add(arrived)
    return result


def local(fixed_image, moving_image, moving_grad):
    plane_count, height, widths = fixed_image.shape
    plane_base = lax.axis_index("gz") * plane_count
    row_base = lax.axis_index("gy") * height
    total_depth = plane_count * lax.axis_size("gz")
    total_height = height * lax.axis_size("gy")
    halo_depth = RADIUS
    stacked = jnp.stack([fixed_image, moving_image])
    images = padded(stacked, (("gz", 1), ("gy", 2)), halo_depth)
    coef_fields = coefficient_fields(images)
    coef_fields = padded(coef_fields, (("gz", 1), ("gy", 2)), RADIUS)
    boxed = box_three(coef_fields, plane_count, height)
    centre = images[:, halo_depth : halo_depth + plane_count, halo_depth : halo_depth + height]
    similarity_slope = -SIM_WEIGHT * (
        centre[0] * boxed[0] - boxed[1] + 2.0 * centre[1] * boxed[2] - 2.0 * boxed[3]
    )
    voxel_grad = similarity_slope[None] * moving_grad
    points_x = widths // SPACING
    basis_x = spline_basis(widths, points_x, 0, 0, points_x)
    along_x = jnp.dot(voxel_grad.reshape(-1, widths), basis_x, precision=lax.Precision.HIGHEST)
    along_x = along_x.reshape(3, plane_count, height, points_x)
    points_y = total_height // SPACING
    basis_y = spline_basis(height, points_y, row_base, 0, points_y)
    along_y = jnp.einsum("cdhx,hy->cdyx", along_x, basis_y, precision=lax.Precision.HIGHEST)
    owned_points = plane_count // SPACING
    basis_z = spline_basis(
        plane_count, total_depth // SPACING, plane_base, plane_base // SPACING - 1, owned_points + 3
    )
    partial_sums = jnp.einsum("cdyx,dq->qcyx", along_y, basis_z, precision=lax.Precision.HIGHEST)
    result = combine_slabs(partial_sums, owned_points)
    result = row_sum(result)
    return result


def solution(mesh):
    in_specs = (P("gz", "gy", None), P("gz", "gy", None), P(None, "gz", "gy", None))
    out_specs = P("gz", None, "gy", None)
    return jax.shard_map(local, mesh=mesh, in_specs=in_specs, out_specs=out_specs, check_vma=False)
```

profile of v0, /device:TPU:1, one launch (start us, length us, event | category | flops | bytes accessed | tf_op | source)
XLA Modules:
  0.0 153.5 jit_solution(15687157971532622886)
XLA Ops:
  0.0 1.5 pad_maximum_fusion.7
  1.5 4.5 %collective-permute-start = (f32[2,4,40,320]{3,2,1,0:T(8,128)S(1)}, f32[2,4,40,320]{3,2,1,0:T(8,128)S(1)}, u32[]{:S(2)}, u32[]{:S(2)}) collective-permute-start(f32[2,4,40,320]{3,2,1,0:T(8,128)S(1)} %get-tuple-element.56), channel_id=1, source_target_pairs={{0,2},{2,4},{4,6},{6,8},{8,10},{10,12},{12,14},{14,16},{16,18},{18... | collective-permute-start | bytes 1228808 | tf_op jit(solution)/shard_map/ppermute | solution.py:27
  6.0 1.9 %collective-permute-start.1 = (f32[2,4,40,320]{3,2,1,0:T(8,128)S(1)}, f32[2,4,40,320]{3,2,1,0:T(8,128)S(1)}, u32[]{:S(2)}, u32[]{:S(2)}) collective-permute-start(f32[2,4,40,320]{3,2,1,0:T(8,128)S(1)} %get-tuple-element.57), channel_id=1, source_target_pairs={{2,0},{4,2},{6,4},{8,6},{10,8},{12,10},{14,12},{16,14},{18,16},{20... | collective-permute-start | bytes 1228808 | tf_op jit(solution)/shard_map/ppermute | solution.py:28
  7.9 9.1 %collective-permute-done = f32[2,4,40,320]{3,2,1,0:T(8,128)S(1)} collective-permute-done((f32[2,4,40,320]{3,2,1,0:T(8,128)S(1)}, f32[2,4,40,320]{3,2,1,0:T(8,128)S(1)}, u32[]{:S(2)}, u32[]{:S(2)}) %collective-permute-start) | collective-permute-done | bytes 409632 | tf_op jit(solution)/shard_map/ppermute | solution.py:27
  17.1 3.1 %collective-permute-start.2 = (f32[2,18,4,320]{3,2,1,0:T(4,128)S(1)}, f32[2,18,4,320]{3,2,1,0:T(4,128)S(1)}, u32[]{:S(2)}, u32[]{:S(2)}) collective-permute-start(f32[2,18,4,320]{3,2,1,0:T(4,128)S(1)} %get-tuple-element.52), channel_id=1, source_target_pairs={{0,1},{2,3},{4,5},{6,7},{8,9},{10,11},{12,13},{14,15},{16,17},{18,... | collective-permute-start | bytes 552968 | tf_op jit(solution)/shard_map/ppermute | solution.py:27
  20.3 1.3 collective-permute-start.3
  21.6 1.5 collective-permute-done.2
  23.1 3.8 %collective-permute-done.3 = f32[2,18,4,320]{3,2,1,0:T(4,128)S(1)} collective-permute-done((f32[2,18,4,320]{3,2,1,0:T(4,128)S(1)}, f32[2,18,4,320]{3,2,1,0:T(4,128)S(1)}, u32[]{:S(2)}, u32[]{:S(2)}) %collective-permute-start.3) | collective-permute-done | bytes 184352 | tf_op jit(solution)/shard_map/ppermute | solution.py:28
  27.8 5.6 %slice_add_fusion.17 = (f32[18,48,320]{2,1,0:T(8,128)S(1)}, f32[18,48,320]{2,1,0:T(8,128)S(1)}) fusion(f32[18,48,320]{2,1,0:T(8,128)S(1)} %get-tuple-element.47, f32[18,48,320]{2,1,0:T(8,128)S(1)} %get-tuple-element.49), kind=kLoop, calls=%fused_computation.28 | loop fusion | flops 4423680 | bytes 4423680 | tf_op jit(solution)/shard_map/add | solution.py:57
  34.2 0.8 slice_add_fusion.30
  35.0 5.6 %slice_add_fusion.19 = (f32[18,48,320]{2,1,0:T(8,128)S(1)}, f32[18,48,320]{2,1,0:T(8,128)S(1)}) fusion(f32[18,48,320]{2,1,0:T(8,128)S(1)} %get-tuple-element.45, f32[18,48,320]{2,1,0:T(8,128)S(1)} %get-tuple-element.46), kind=kLoop, calls=%fused_computation.40 | loop fusion | flops 4423680 | bytes 4423680 | tf_op jit(solution)/shard_map/add | solution.py:57
  42.2 2.8 %slice_add_fusion.21 = f32[18,48,320]{2,1,0:T(8,128)S(1)} fusion(f32[18,48,320]{2,1,0:T(8,128)S(1)} %get-tuple-element.48), kind=kLoop, calls=%fused_computation.52 | loop fusion | flops 2211840 | bytes 2211840 | tf_op jit(solution)/shard_map/add | solution.py:57
  45.8 2.6 %multiply_bitcast_fusion.2 = (f32[1,10,40,320]{3,2,1,0:T(8,128)S(1)}, f32[10,40,320]{2,1,0:T(8,128)S(1)}, f32[10,40,320]{2,1,0:T(8,128)S(1)}, f32[10,40,320]{2,1...) fusion(f32[18,40,320]{2,1,0:T(8,128)S(1)} %slice_add_fusion.30, ...), kind=kLoop, calls=%fused_computation.164 | loop fusion | flops 6912000 | bytes 26112000 | tf_op jit(solution)/shard_map/stack | solution.py:86
  48.7 1.5 pad_maximum_fusion.5
  50.2 6.2 %collective-permute-start.4 = (f32[4,4,40,320]{3,2,1,0:T(8,128)}, f32[4,4,40,320]{3,2,1,0:T(8,128)}, u32[]{:S(2)}, u32[]{:S(2)}) collective-permute-start(f32[4,4,40,320]{3,2,1,0:T(8,128)} %get-tuple-element.50), channel_id=1, source_target_pairs={{0,2},{2,4},{4,6},{6,8},{8,10},{10,12},{12,14},{14,16},{16,18},{18... | collective-permute-start | bytes 2457608 | tf_op jit(solution)/shard_map/ppermute | solution.py:27
  56.4 1.9 %collective-permute-start.5 = (f32[4,4,40,320]{3,2,1,0:T(8,128)}, f32[4,4,40,320]{3,2,1,0:T(8,128)}, u32[]{:S(2)}, u32[]{:S(2)}) collective-permute-start(f32[4,4,40,320]{3,2,1,0:T(8,128)} %get-tuple-element.51), channel_id=1, source_target_pairs={{2,0},{4,2},{6,4},{8,6},{10,8},{12,10},{14,12},{16,14},{18,16},{20... | collective-permute-start | bytes 2457608 | tf_op jit(solution)/shard_map/ppermute | solution.py:28
  62.4 15.9 %collective-permute-done.4 = f32[4,4,40,320]{3,2,1,0:T(8,128)} collective-permute-done((f32[4,4,40,320]{3,2,1,0:T(8,128)}, f32[4,4,40,320]{3,2,1,0:T(8,128)}, u32[]{:S(2)}, u32[]{:S(2)}) %collective-permute-start.4) | collective-permute-done | bytes 819232 | tf_op jit(solution)/shard_map/ppermute | solution.py:27
  78.3 2.2 %pad_maximum_fusion.13 = (f32[4,18,4,320]{3,2,1,0:T(4,128)}, f32[4,18,4,320]{3,2,1,0:T(4,128)S(1)}) fusion(f32[4,4,40,320]{3,2,1,0:T(8,128)} %collective-permute-done.5, f32[4,4,40,320]{3,2,1,0:T(8,128)} %collective-permute-done.4, f32[1,10,40,320]{3,2,1,0:T(8,128)S(1)} %get-tuple-element.55, f32[1,10,40,320]{3,2,1,0:T(8,128)S(1)} %get-tuple-element.54, ...), kind=kLoop, calls=%fused_computation.172 | loop fusion | flops 921600 | bytes 4423680 | tf_op jit(solution)/shard_map/slice | solution.py:25
  80.5 2.1 %collective-permute-start.6 = (f32[4,18,4,320]{3,2,1,0:T(4,128)}, f32[4,18,4,320]{3,2,1,0:T(4,128)}, u32[]{:S(2)}, u32[]{:S(2)}) collective-permute-start(f32[4,18,4,320]{3,2,1,0:T(4,128)} %get-tuple-element.43), channel_id=1, source_target_pairs={{0,1},{2,3},{4,5},{6,7},{8,9},{10,11},{12,13},{14,15},{16,17},{18,... | collective-permute-start | bytes 1105928 | tf_op jit(solution)/shard_map/ppermute | solution.py:27
  82.6 1.3 collective-permute-start.7
  85.6 1.7 %collective-permute-done.6 = f32[4,18,4,320]{3,2,1,0:T(4,128)} collective-permute-done((f32[4,18,4,320]{3,2,1,0:T(4,128)}, f32[4,18,4,320]{3,2,1,0:T(4,128)}, u32[]{:S(2)}, u32[]{:S(2)}) %collective-permute-start.6) | collective-permute-done | bytes 368672 | tf_op jit(solution)/shard_map/ppermute | solution.py:27
  87.4 4.4 %collective-permute-done.7 = f32[4,18,4,320]{3,2,1,0:T(4,128)} collective-permute-done((f32[4,18,4,320]{3,2,1,0:T(4,128)S(1)}, f32[4,18,4,320]{3,2,1,0:T(4,128)}, u32[]{:S(2)}, u32[]{:S(2)}) %collective-permute-start.7) | collective-permute-done | bytes 368672 | tf_op jit(solution)/shard_map/ppermute | solution.py:28
  91.8 5.8 %pad_maximum_fusion = f32[4,18,48,320]{3,2,1,0:T(8,128)} fusion(f32[4,18,4,320]{3,2,1,0:T(4,128)} %collective-permute-done.7, f32[4,4,40,320]{3,2,1,0:T(8,128)} %collective-permute-done.5, f32[1,10,40,320]{3,2,1,0:T(8,128)S(1)} %get-tuple-element.55, f32[1,10,40,320]{3,2,1,0:T(8,128)S(1)} %get-tuple-element.54, f32[1,10,40,320]{3,2,1,0:T(8,128)} %copy-done.2, ...), kind=kLoop, calls=%fused_computation | loop fusion | flops 7741440 | bytes 8847360 | tf_op jit(solution)/shard_map/concatenate | solution.py:29
  97.5 21.9 %slice_add_fusion = f32[4,18,48,320]{3,2,1,0:T(8,128)S(1)} fusion(f32[4,18,48,320]{3,2,1,0:T(8,128)} %pad_maximum_fusion), kind=kLoop, calls=%fused_computation.1 | loop fusion | flops 8847360 | bytes 8847360 | tf_op jit(solution)/shard_map/add | solution.py:57
  119.4 4.6 %slice_add_fusion.1 = f32[4,18,40,320]{3,2,1,0:T(8,128)} fusion(f32[4,18,48,320]{3,2,1,0:T(8,128)S(1)} %slice_add_fusion), kind=kLoop, calls=%fused_computation.7 | loop fusion | flops 7372800 | bytes 36864000 | tf_op jit(solution)/shard_map/add | solution.py:57
  124.0 9.8 %slice_add_fusion.9 = f32[4,10,40,320]{3,2,1,0:T(8,128)S(1)} fusion(f32[4,18,40,320]{3,2,1,0:T(8,128)} %slice_add_fusion.1), kind=kLoop, calls=%fused_computation.16 | loop fusion | flops 4096000 | bytes 20480000 | tf_op jit(solution)/shard_map/add | solution.py:57
  134.1 1.3 copy-done.3
  135.5 2.0 %fusion.2 = f32[3,10,40,64]{3,2,1,0:T(8,128)S(1)} fusion(f32[3,10,40,320]{3,2,1,0:T(8,128)S(1)} %copy-done.3, f32[10,40,320]{2,1,0:T(8,128)S(1)} %fusion.17, f32[320]{0:T(512)S(1)} %get-tuple-element.68, s32[320]{0:T(512)S(1)} %get-tuple-element.69, f32[320]{0:T(512)S(1)} %get-tuple-element.66, s32[320]{0:T(512)S(1)} %get-tuple-element.70, ...), kind=kOutput, calls=%fused_computation.24 | convolution fusion | flops 295521280 | bytes 2365440 | tf_op jit(solution)/shard_map/dot_general | solution.py:140
  138.6 1.9 %collective-permute-start.8 = (f32[1,3,16,64]{3,0,2,1:T(1,128)S(1)}, f32[1,3,16,64]{3,0,2,1:T(1,128)S(1)}, u32[]{:S(2)}, u32[]{:S(2)}) collective-permute-start(f32[1,3,16,64]{3,0,2,1:T(1,128)S(1)} %slice.869), channel_id=1, source_target_pairs={{2,0},{4,2},{6,4},{8,6},{10,8},{12,10},{14,12},{16,14},{18,16},{20... | collective-permute-start | bytes 36872 | tf_op jit(solution)/shard_map/ppermute | solution.py:17
  140.6 5.7 %collective-permute-start.9 = (f32[2,3,16,64]{3,0,2,1:T(2,128)S(1)}, f32[2,3,16,64]{3,0,2,1:T(2,128)S(1)}, u32[]{:S(2)}, u32[]{:S(2)}) collective-permute-start(f32[2,3,16,64]{3,0,2,1:T(2,128)S(1)} %get-tuple-element.59), channel_id=1, source_target_pairs={{0,2},{2,4},{4,6},{6,8},{8,10},{10,12},{12,14},{14,16},{16,18},{18... | collective-permute-start | bytes 73736 | tf_op jit(solution)/shard_map/ppermute | solution.py:17
  146.5 1.0 collective-permute-done.9
  147.5 5.4 %all-reduce.6 = f32[2,3,16,64]{3,0,2,1:T(2,128)S(1)} all-reduce(f32[2,3,16,64]{3,0,2,1:T(2,128)S(1)} %add.1035), channel_id=2, replica_groups=mesh['gz'=16,'gy'=2] {'gy'}, use_global_device_ids=true, to_apply=%region_0.1.clone | all-reduce | flops 6144 | bytes 49152
  (75 shorter events, 11.7 us)
Async XLA Ops:
  0.0 17.0 %copy-start.1 = (f32[10,40,320]{2,1,0:T(8,128)S(1)}, f32[10,40,320]{2,1,0:T(8,128)}, u32[]{:S(2)}) copy-start(f32[10,40,320]{2,1,0:T(8,128)} %param.9) | copy-start | bytes 1536004
  0.0 17.0 %copy-start = (f32[10,40,320]{2,1,0:T(8,128)S(1)}, f32[10,40,320]{2,1,0:T(8,128)}, u32[]{:S(2)}) copy-start(f32[10,40,320]{2,1,0:T(8,128)} %param.10) | copy-start | bytes 1536004
  1.5 15.6 %collective-permute-start = (f32[2,4,40,320]{3,2,1,0:T(8,128)S(1)}, f32[2,4,40,320]{3,2,1,0:T(8,128)S(1)}, u32[]{:S(2)}, u32[]{:S(2)}) collective-permute-start(f32[2,4,40,320]{3,2,1,0:T(8,128)S(1)} %get-tuple-element.56), channel_id=1, source_target_pairs={{0,2},{2,4},{4,6},{6,8},{8,10},{10,12},{12,14},{14,16},{16,18},{18... | collective-permute-start | bytes 1228808 | tf_op jit(solution)/shard_map/ppermute | solution.py:27
  6.0 11.0 %collective-permute-start.1 = (f32[2,4,40,320]{3,2,1,0:T(8,128)S(1)}, f32[2,4,40,320]{3,2,1,0:T(8,128)S(1)}, u32[]{:S(2)}, u32[]{:S(2)}) collective-permute-start(f32[2,4,40,320]{3,2,1,0:T(8,128)S(1)} %get-tuple-element.57), channel_id=1, source_target_pairs={{2,0},{4,2},{6,4},{8,6},{10,8},{12,10},{14,12},{16,14},{18,16},{20... | collective-permute-start | bytes 1228808 | tf_op jit(solution)/shard_map/ppermute | solution.py:28
  17.1 6.0 %collective-permute-start.2 = (f32[2,18,4,320]{3,2,1,0:T(4,128)S(1)}, f32[2,18,4,320]{3,2,1,0:T(4,128)S(1)}, u32[]{:S(2)}, u32[]{:S(2)}) collective-permute-start(f32[2,18,4,320]{3,2,1,0:T(4,128)S(1)} %get-tuple-element.52), channel_id=1, source_target_pairs={{0,1},{2,3},{4,5},{6,7},{8,9},{10,11},{12,13},{14,15},{16,17},{18,... | collective-permute-start | bytes 552968 | tf_op jit(solution)/shard_map/ppermute | solution.py:27
  20.3 6.7 %collective-permute-start.3 = (f32[2,18,4,320]{3,2,1,0:T(4,128)S(1)}, f32[2,18,4,320]{3,2,1,0:T(4,128)S(1)}, u32[]{:S(2)}, u32[]{:S(2)}) collective-permute-start(f32[2,18,4,320]{3,2,1,0:T(4,128)S(1)} %get-tuple-element.53), channel_id=1, source_target_pairs={{1,0},{3,2},{5,4},{7,6},{9,8},{11,10},{13,12},{15,14},{17,16},{19,... | collective-permute-start | bytes 552968 | tf_op jit(solution)/shard_map/ppermute | solution.py:28
  48.7 1.5 %copy-start.2 = (f32[1,10,40,320]{3,2,1,0:T(8,128)}, f32[1,10,40,320]{3,2,1,0:T(8,128)S(1)}, u32[]{:S(2)}) copy-start(f32[1,10,40,320]{3,2,1,0:T(8,128)S(1)} %get-tuple-element.58) | copy-start | bytes 1536004
  50.2 28.1 %collective-permute-start.4 = (f32[4,4,40,320]{3,2,1,0:T(8,128)}, f32[4,4,40,320]{3,2,1,0:T(8,128)}, u32[]{:S(2)}, u32[]{:S(2)}) collective-permute-start(f32[4,4,40,320]{3,2,1,0:T(8,128)} %get-tuple-element.50), channel_id=1, source_target_pairs={{0,2},{2,4},{4,6},{6,8},{8,10},{10,12},{12,14},{14,16},{16,18},{18... | collective-permute-start | bytes 2457608 | tf_op jit(solution)/shard_map/ppermute | solution.py:27
  56.4 21.9 %collective-permute-start.5 = (f32[4,4,40,320]{3,2,1,0:T(8,128)}, f32[4,4,40,320]{3,2,1,0:T(8,128)}, u32[]{:S(2)}, u32[]{:S(2)}) collective-permute-start(f32[4,4,40,320]{3,2,1,0:T(8,128)} %get-tuple-element.51), channel_id=1, source_target_pairs={{2,0},{4,2},{6,4},{8,6},{10,8},{12,10},{14,12},{16,14},{18,16},{20... | collective-permute-start | bytes 2457608 | tf_op jit(solution)/shard_map/ppermute | solution.py:28
  62.4 22.0 %copy-start.19 = (u32[32]{0:T(128)S(1)}, u32[32]{0:T(128)}, u32[]{:S(2)}) copy-start(u32[32]{0:T(128)} %constant.222) | copy-start | bytes 388
  80.5 6.8 %collective-permute-start.6 = (f32[4,18,4,320]{3,2,1,0:T(4,128)}, f32[4,18,4,320]{3,2,1,0:T(4,128)}, u32[]{:S(2)}, u32[]{:S(2)}) collective-permute-start(f32[4,18,4,320]{3,2,1,0:T(4,128)} %get-tuple-element.43), channel_id=1, source_target_pairs={{0,1},{2,3},{4,5},{6,7},{8,9},{10,11},{12,13},{14,15},{16,17},{18,... | collective-permute-start | bytes 1105928 | tf_op jit(solution)/shard_map/ppermute | solution.py:27
  82.6 9.1 %collective-permute-start.7 = (f32[4,18,4,320]{3,2,1,0:T(4,128)S(1)}, f32[4,18,4,320]{3,2,1,0:T(4,128)}, u32[]{:S(2)}, u32[]{:S(2)}) collective-permute-start(f32[4,18,4,320]{3,2,1,0:T(4,128)S(1)} %get-tuple-element.44), channel_id=1, source_target_pairs={{1,0},{3,2},{5,4},{7,6},{9,8},{11,10},{13,12},{15,14},{17,16},{19,... | collective-permute-start | bytes 1105928 | tf_op jit(solution)/shard_map/ppermute | solution.py:28
  133.8 1.5 copy-start.3
  135.4 2.1 %copy-start.4 = (s32[40]{0:T(128)S(1)}, s32[40]{0:T(128)}, u32[]{:S(2)}) copy-start(s32[40]{0:T(128)} %get-tuple-element.75) | copy-start | bytes 484
  135.4 2.1 %copy-start.5 = (s32[40]{0:T(128)S(1)}, s32[40]{0:T(128)}, u32[]{:S(2)}) copy-start(s32[40]{0:T(128)} %get-tuple-element.76) | copy-start | bytes 484
  135.4 2.1 %copy-start.12 = (f32[40]{0:T(128)S(1)}, f32[40]{0:T(128)}, u32[]{:S(2)}) copy-start(f32[40]{0:T(128)} %get-tuple-element.77) | copy-start | bytes 484
  135.4 2.1 %copy-start.13 = (f32[40]{0:T(128)S(1)}, f32[40]{0:T(128)}, u32[]{:S(2)}) copy-start(f32[40]{0:T(128)} %get-tuple-element.78) | copy-start | bytes 484
  135.4 2.1 %copy-start.16 = (s32[40]{0:T(128)S(1)}, s32[40]{0:T(128)}, u32[]{:S(2)}) copy-start(s32[40]{0:T(128)} %get-tuple-element.79) | copy-start | bytes 484
  135.4 2.1 %copy-start.17 = (s32[40]{0:T(128)S(1)}, s32[40]{0:T(128)}, u32[]{:S(2)}) copy-start(s32[40]{0:T(128)} %get-tuple-element.80) | copy-start | bytes 484
  135.4 2.7 %copy-start.6 = (f32[10]{0:T(128)S(1)}, f32[10]{0:T(128)}, u32[]{:S(2)}) copy-start(f32[10]{0:T(128)} %get-tuple-element.81) | copy-start | bytes 124
  135.4 2.7 %copy-start.7 = (f32[10]{0:T(128)S(1)}, f32[10]{0:T(128)}, u32[]{:S(2)}) copy-start(f32[10]{0:T(128)} %get-tuple-element.82) | copy-start | bytes 124
  135.4 2.7 %copy-start.8 = (s32[10]{0:T(128)S(1)}, s32[10]{0:T(128)}, u32[]{:S(2)}) copy-start(s32[10]{0:T(128)} %get-tuple-element.83) | copy-start | bytes 124
  135.4 2.7 %copy-start.9 = (s32[10]{0:T(128)S(1)}, s32[10]{0:T(128)}, u32[]{:S(2)}) copy-start(s32[10]{0:T(128)} %get-tuple-element.84) | copy-start | bytes 124
  135.4 2.7 %copy-start.10 = (f32[10]{0:T(128)S(1)}, f32[10]{0:T(128)}, u32[]{:S(2)}) copy-start(f32[10]{0:T(128)} %get-tuple-element.85) | copy-start | bytes 124
  135.4 2.7 %copy-start.11 = (f32[10]{0:T(128)S(1)}, f32[10]{0:T(128)}, u32[]{:S(2)}) copy-start(f32[10]{0:T(128)} %get-tuple-element.86) | copy-start | bytes 124
  135.4 2.7 %copy-start.14 = (s32[10]{0:T(128)S(1)}, s32[10]{0:T(128)}, u32[]{:S(2)}) copy-start(s32[10]{0:T(128)} %get-tuple-element.87) | copy-start | bytes 124
  135.5 2.7 %copy-start.15 = (s32[10]{0:T(128)S(1)}, s32[10]{0:T(128)}, u32[]{:S(2)}) copy-start(s32[10]{0:T(128)} %get-tuple-element.88) | copy-start | bytes 124
  135.5 2.7 %copy-start.18 = (s32[5]{0:T(128)S(1)}, s32[5]{0:T(128)}, u32[]{:S(2)}) copy-start(s32[5]{0:T(128)} %iota_add_fusion.1) | copy-start | bytes 64
  138.6 7.7 %collective-permute-start.8 = (f32[1,3,16,64]{3,0,2,1:T(1,128)S(1)}, f32[1,3,16,64]{3,0,2,1:T(1,128)S(1)}, u32[]{:S(2)}, u32[]{:S(2)}) collective-permute-start(f32[1,3,16,64]{3,0,2,1:T(1,128)S(1)} %slice.869), channel_id=1, source_target_pairs={{2,0},{4,2},{6,4},{8,6},{10,8},{12,10},{14,12},{16,14},{18,16},{20... | collective-permute-start | bytes 36872 | tf_op jit(solution)/shard_map/ppermute | solution.py:17
  140.6 6.9 %collective-permute-start.9 = (f32[2,3,16,64]{3,0,2,1:T(2,128)S(1)}, f32[2,3,16,64]{3,0,2,1:T(2,128)S(1)}, u32[]{:S(2)}, u32[]{:S(2)}) collective-permute-start(f32[2,3,16,64]{3,0,2,1:T(2,128)S(1)} %get-tuple-element.59), channel_id=1, source_target_pairs={{0,2},{2,4},{4,6},{6,8},{8,10},{10,12},{12,14},{14,16},{16,18},{18... | collective-permute-start | bytes 73736 | tf_op jit(solution)/shard_map/ppermute | solution.py:17
where the time goes:
time: 156 us; the launch traced here: 154 us
  other arithmetic  73.8 us (47%)
  waiting for transfers between devices  37.4 us (24%)
  starting transfers between devices  30 us (19%)
  blocking collectives  5.41 us (3%)
  matrix products  2.95 us (2%)
  local copies, waits for them, and re-layouts  2.91 us (2%)
    add x11, other arithmetic, box_along(): running + lax.slice_in_dim(values, offset, offset + length, axis=dimension)  54.3 us
    ppermute x4, waiting for transfers between devices, padded(): before = lax.ppermute(last, axis, up)  28.2 us
    ppermute x4, starting transfers between devices, padded(): before = lax.ppermute(last, axis, up)  15.9 us
    ppermute x4, waiting for transfers between devices, padded(): after = lax.ppermute(leading, axis, down)  8.23 us
    ppermute x2, starting transfers between devices, passed_along(): return lax.ppermute(block, axis, route)  7.62 us
    ppermute x4, starting transfers between devices, padded(): after = lax.ppermute(leading, axis, down)  6.41 us
    concatenate x2, other arithmetic, padded(): shard = jnp.concatenate([before, shard, after], axis=dim)  6.06 us
    unnamed x1, blocking collectives  5.41 us
  transfers between devices with their start and end apart: 10, of which 7 were waited for; matrix products, arithmetic and copies ran while one was open for 4% of the time, Pallas kernels for 0%

commit v1 on v0

v1 whole, which is shorter than its diff:
```python
import functools

import jax
import jax.numpy as jnp
import numpy as np
from jax import lax
from jax.experimental import pallas as pl
from jax.experimental.pallas import tpu as pltpu
from jax.sharding import PartitionSpec as P

RADIUS = 4
SPACING = 5
EPS = 36.0
SIM_WEIGHT = 8.0
WINDOW = float((2 * RADIUS + 1) ** 3)
HALO = 2 * RADIUS
MESH = pl.DeviceIdType.MESH


def spline_matrix(voxels, points):
    position = np.arange(voxels)
    cell = position // SPACING
    u = (position - cell * SPACING) / SPACING
    weights = [
        (1 - u) ** 3 / 6,
        (3 * u**3 - 6 * u**2 + 4) / 6,
        (-3 * u**3 + 3 * u**2 + 3 * u + 1) / 6,
        u**3 / 6,
    ]
    matrix = np.zeros((voxels, points))
    for k in range(4):
        np.add.at(matrix, (position, np.clip(cell - 1 + k, 0, points - 1)), weights[k])
    return matrix


def window_sum(v, axis, leading):
    n = v.shape[axis]

    def moved(a, s):
        return pltpu.roll(a, n - s if leading else s, axis)

    two = v + moved(v, 1)
    four = two + moved(two, 2)
    eight = four + moved(four, 4)
    return eight + moved(v, 8)


def split(v):
    hi = v.astype(jnp.bfloat16)
    return hi, (v - hi.astype(jnp.float32)).astype(jnp.bfloat16)


def dot(a, b):
    return jnp.dot(a, b, preferred_element_type=jnp.float32)


def kernel(
    gz_count, planes, height, width, points_y, points_x,
    bz_ref, fixed_ref, moving_ref, grad_ref, bx_ref, by_ref, out_ref,
    ext, grad, sums, boxes, coef, ksum, slope, acc, part, arrived,
    local_sem, z_send, z_recv, y_send, y_recv, p_send, p_recv,
):
    z, g = lax.axis_index("gz"), lax.axis_index("gy")
    other = 1 - g
    up, down = z < gz_count - 1, z > 0
    rows, lanes = slope.shape
    y0 = pl.multiple_of(g * HALO, 8)
    y_src = pl.multiple_of(jnp.where(g == 0, height - HALO, HALO), 8)
    y_dst = pl.multiple_of(jnp.where(g == 0, 0, height), 8)
    own_src = pl.multiple_of(jnp.where(g == 0, height - HALO, 0), 8)
    owned = planes // SPACING
    cols = owned + 3
    images = (fixed_ref, moving_ref)

    def window(p, i):
        return ext.at[i, p, pl.ds(y0, height)]

    local = [
        pltpu.make_async_copy(
            images[i],
            ext.at[i, pl.ds(HALO, planes), pl.ds(y0, height)],
            local_sem.at[i],
        )
        for i in range(2)
    ] + [pltpu.make_async_copy(grad_ref, grad, local_sem.at[2])]

    ext[:, :, rows - 8 :, :] = jnp.zeros((2, ext.shape[1], 8, width), jnp.float32)

    @pl.when(jnp.logical_not(down))
    def _():
        ext[:, 0:HALO] = jnp.zeros((2, HALO, rows, width), jnp.float32)

    @pl.when(jnp.logical_not(up))
    def _():
        ext[:, HALO + planes :] = jnp.zeros((2, HALO, rows, width), jnp.float32)

    barrier = pltpu.get_barrier_semaphore()

    def greet(cond, dz, gy):
        @pl.when(cond)
        def _():
            pl.semaphore_signal(barrier, 1, device_id={"gz": z + dz, "gy": gy}, device_id_type=MESH)

    pl.semaphore_signal(barrier, 1, device_id={"gz": z, "gy": other}, device_id_type=MESH)
    for gy in (g, other):
        greet(up, 1, gy)
        greet(down, -1, gy)
    pl.semaphore_wait(barrier, 1 + 2 * up.astype(jnp.int32) + 2 * down.astype(jnp.int32))

    def z_copy(i, d, s):
        src = planes - 1 - s if d == 0 else s
        dst = HALO - 1 - s if d == 0 else HALO + planes + s
        return pltpu.make_async_remote_copy(
            images[i].at[src], window(dst, i),
            z_send.at[i, d, s], z_recv.at[i, d, s],
            device_id={"gz": z + 1 if d == 0 else z - 1, "gy": g}, device_id_type=MESH,
        )

    def y_own(i):
        return pltpu.make_async_remote_copy(
            images[i].at[:, pl.ds(own_src, HALO), :],
            ext.at[i, pl.ds(HALO, planes), pl.ds(y_dst, HALO)],
            y_send.at[2, i], y_recv.at[2, i],
            device_id={"gz": z, "gy": other}, device_id_type=MESH,
        )

    def y_relay(d, s):
        p = HALO - 1 - s if d == 0 else HALO + planes + s
        return pltpu.make_async_remote_copy(
            ext.at[:, p, pl.ds(y_src, HALO)],
            ext.at[:, p, pl.ds(y_dst, HALO)],
            y_send.at[d, s], y_recv.at[d, s],
            device_id={"gz": z, "gy": other}, device_id_type=MESH,
        )

    sends = (up, down)
    takes = (down, up)

    for i in range(2):
        local[i].start()
        y_own(i).start()
    for d in range(2):
        @pl.when(sends[d])
        def _():
            for s in range(HALO):
                for i in range(2):
                    z_copy(i, d, s).start()
    local[2].start()
    for i in range(2):
        local[i].wait()
        y_own(i).wait_recv()

    def relay(s):
        for d in range(2):
            @pl.when(takes[d])
            def _():
                for i in range(2):
                    z_copy(i, d, s).wait_recv()
                y_relay(d, s).start()

    def ready(d, s):
        @pl.when(takes[d])
        def _():
            y_relay(d, s).wait_recv()

    pad = jnp.zeros((rows, lanes - width), jnp.float32)

    def plane(i, p):
        return jnp.concatenate([ext[i, p], pad], axis=1)

    def fields(p):
        f, m = plane(0, p), plane(1, p)
        return f, m, f * f, m * m, f * m

    row = lax.broadcasted_iota(jnp.int32, (rows, lanes), 0)
    lane = lax.broadcasted_iota(jnp.int32, (rows, lanes), 1)
    inside = (row >= RADIUS) & (row < rows - RADIUS) & (lane >= RADIUS) & (lane < width + RADIUS)

    def coefficients(way, k):
        for i in range(5):
            boxes[i] = window_sum(window_sum(sums[way, i], 0, False), 1, False)
        sf, sm = boxes[0], boxes[1]
        cov = boxes[4] - sf * sm * (1.0 / WINDOW)
        var_f = boxes[2] - sf * sf * (1.0 / WINDOW) + EPS
        var_m = boxes[3] - sm * sm * (1.0 / WINDOW) + EPS
        at = z * planes + k - RADIUS
        valid = (at >= 0) & (at < gz_count * planes)
        keep = jnp.where(valid, 1.0, 0.0)
        inv = 1.0 / (var_f * var_m)
        q = jnp.where(inside, cov * inv * keep, 0.0)
        h = q * cov * (var_f * inv)
        coef[0, k] = q
        coef[1, k] = h
        coef[2, k] = (q * sf - h * sm) * (1.0 / WINDOW)

    for i in range(5):
        sums[0, i] = jnp.zeros((rows, lanes), jnp.float32)

    @pl.loop(0, HALO + 1)
    def _(p):
        for i, v in enumerate(fields(HALO + p)):
            sums[0, i] += v

    sums[1] = sums[0]
    coefficients(0, HALO)

    def move(way, new, old, k):
        for i, (a, b) in enumerate(zip(fields(new), fields(old))):
            sums[way, i] += a - b
        coefficients(way, k)

    first = planes - 1 - HALO
    for j in range(first):
        move(0, 2 * HALO + 1 + j, HALO + j, HALO + 1 + j)

    relay(0)

    @pl.loop(0, HALO)
    def _(s):
        @pl.when(s < HALO - 1)
        def _():
            relay(s + 1)

        ready(0, s)
        move(1, HALO - 1 - s, 2 * HALO - s, HALO - 1 - s)
        ready(1, s)
        move(0, HALO + planes + s, planes - 1 + s, planes + s)

    for i in range(3):
        ksum[i] = jnp.zeros((rows, lanes), jnp.float32)
    acc[...] = jnp.zeros(acc.shape, jnp.float32)

    @pl.loop(0, HALO)
    def _(k):
        for i in range(3):
            ksum[i] += coef[i, k]

    local[2].wait()
    for cell in range(owned):
        @pl.loop(cell * SPACING, (cell + 1) * SPACING)
        def _(o):
            boxed = []
            for i in range(3):
                total = ksum[i] + coef[i, o + HALO]
                ksum[i] = total - coef[i, o]
                boxed.append(window_sum(window_sum(total, 0, True), 1, True))
            slope[...] = (-2.0 * SIM_WEIGHT) * (
                plane(0, o + HALO) * boxed[0] - plane(1, o + HALO) * boxed[1] - boxed[2]
            )
            own = slope[pl.ds(y0, height), 0:width]
            for c in range(3):
                v = own * grad[c, o]
                for j in range(cell, cell + 4):
                    acc[c * cols + j] += bz_ref[z * planes + o, j] * v

    for c in range(3):
        v = acc[c * cols : (c + 1) * cols].reshape(cols * height, width)
        hi, lo = split(v)
        along_x = dot(hi, bx_ref[0]) + dot(hi, bx_ref[1]) + dot(lo, bx_ref[0])
        hi, lo = split(along_x)
        by_hi, by_lo = by_ref[g, 0], by_ref[g, 1]
        along_y = dot(by_hi, hi) + dot(by_lo, hi) + dot(by_hi, lo)
        half = points_y // 2
        for j in range(cols):
            for h in range(2):
                at = j * points_y + h * half
                part[h, j, c] = along_y[at : at + half]

    def p_copy(slot, half, first_row, count, dz, gy):
        return pltpu.make_async_remote_copy(
            part.at[half, pl.ds(first_row, count)],
            arrived.at[slot, pl.ds(0, count)],
            p_send.at[slot], p_recv.at[slot],
            device_id={"gz": z + dz, "gy": gy}, device_id_type=MESH,
        )

    partner = p_copy(0, other, 1, owned, 0, other)
    ups = [p_copy(1, g, 1 + owned, 2, 1, g), p_copy(2, other, 1 + owned, 2, 1, other)]
    downs = [p_copy(3, g, 0, 1, -1, g), p_copy(4, other, 0, 1, -1, other)]

    @pl.when(up)
    def _():
        for copy in ups:
            copy.start()

    @pl.when(down)
    def _():
        for copy in downs:
            copy.start()

    partner.start()
    partner.wait_recv()
    out_ref[...] = part[g, 1 : 1 + owned] + arrived[0]

    @pl.when(down)
    def _():
        for copy in ups:
            copy.wait_recv()
        out_ref[0:2] += arrived[1, 0:2] + arrived[2, 0:2]

    @pl.when(up)
    def _():
        for copy in downs:
            copy.wait_recv()
        out_ref[owned - 1 : owned] += arrived[3, 0:1] + arrived[4, 0:1]

    partner.wait_send()
    for i in range(2):
        y_own(i).wait_send()

    @pl.when(up)
    def _():
        for copy in ups:
            copy.wait_send()

    @pl.when(down)
    def _():
        for copy in downs:
            copy.wait_send()

    for d in range(2):
        @pl.when(sends[d])
        def _():
            for s in range(HALO):
                for i in range(2):
                    z_copy(i, d, s).wait_send()

        @pl.when(takes[d])
        def _():
            for s in range(HALO):
                y_relay(d, s).wait_send()


def hi_lo(matrix):
    hi = matrix.astype(jnp.bfloat16)
    lo = (matrix - hi.astype(np.float64)).astype(jnp.bfloat16)
    return np.stack([hi, lo])


def local(gz_count, gy_count, fixed_image, moving_image, moving_grad):
    planes, height, width = fixed_image.shape
    points_x, points_y = width // SPACING, gy_count * height // SPACING
    depth = gz_count * planes
    owned = planes // SPACING
    cols = owned + 3
    assert gy_count == 2 and planes >= HALO + 1 and owned >= 2 and height % 8 == 0
    bx = hi_lo(spline_matrix(width, points_x))
    by_all = spline_matrix(gy_count * height, points_y)
    by = np.stack(
        [hi_lo(np.kron(np.eye(cols), by_all[h * height : (h + 1) * height].T)) for h in range(2)]
    )
    bz_all = np.pad(spline_matrix(depth, depth // SPACING), ((0, 0), (1, 2)))
    bz = np.stack(
        [bz_all[p, (p // planes) * owned : (p // planes) * owned + cols] for p in range(depth)]
    ).astype(np.float32)
    rows = height + 2 * HALO
    lanes = (width + HALO + 127) // 128 * 128
    ext_planes = planes + 2 * HALO
    f32 = jnp.float32
    body = functools.partial(kernel, gz_count, planes, height, width, points_y, points_x)
    vmem, smem, anyw = (pl.BlockSpec(memory_space=m) for m in (pltpu.VMEM, pltpu.SMEM, pl.ANY))
    half = points_y // 2
    return pl.pallas_call(
        body,
        out_shape=jax.ShapeDtypeStruct((owned, 3, half, points_x), f32),
        in_specs=[smem, anyw, anyw, anyw, vmem, vmem],
        out_specs=vmem,
        scratch_shapes=[
            pltpu.VMEM((2, ext_planes, rows, width), f32),
            pltpu.VMEM(moving_grad.shape, f32),
            pltpu.VMEM((2, 5, rows, lanes), f32),
            pltpu.VMEM((5, rows, lanes), f32),
            pltpu.VMEM((3, planes + HALO, rows, lanes), f32),
            pltpu.VMEM((3, rows, lanes), f32),
            pltpu.VMEM((rows, lanes), f32),
            pltpu.VMEM((3 * cols, height, width), f32),
            pltpu.VMEM((2, cols, 3, half, points_x), f32),
            pltpu.VMEM((5, owned, 3, half, points_x), f32),
            pltpu.SemaphoreType.DMA((3,)),
            pltpu.SemaphoreType.DMA((2, 2, HALO)),
            pltpu.SemaphoreType.DMA((2, 2, HALO)),
            pltpu.SemaphoreType.DMA((3, HALO)),
            pltpu.SemaphoreType.DMA((3, HALO)),
            pltpu.SemaphoreType.DMA((5,)),
            pltpu.SemaphoreType.DMA((5,)),
        ],
        compiler_params=pltpu.CompilerParams(
            collective_id=0, has_side_effects=True, vmem_limit_bytes=40 * 2**20
        ),
    )(jnp.asarray(bz), fixed_image, moving_image, moving_grad, jnp.asarray(bx), jnp.asarray(by))


def solution(mesh):
    in_specs = (P("gz", "gy", None), P("gz", "gy", None), P(None, "gz", "gy", None))
    out_specs = P("gz", None, "gy", None)
    body = functools.partial(local, mesh.shape["gz"], mesh.shape["gy"])
    return jax.shard_map(body, mesh=mesh, in_specs=in_specs, out_specs=out_specs, check_vma=False)
```

time: 156 us -> 59.8 us (0.38); the launches traced: 154 us -> 59.5 us
  other arithmetic: 73.8 us -> 0 us
  Pallas kernels: 0 us -> 52.5 us
  waiting for transfers between devices: 37.4 us -> 0 us
  starting transfers between devices: 30 us -> 0 us
  blocking collectives: 5.41 us -> 0 us
  local copies, waits for them, and re-layouts: 2.91 us -> 6.97 us
  matrix products: 2.95 us -> 0 us
    add x14 -> x0, other arithmetic: 54.9 us -> none  [the longest x11 54.3 us: box_along(): running + lax.slice_in_dim(values, offset, offset + length, axis=dimension)]
    pallas_call x0 -> x1, Pallas kernels: none -> 52.5 us  [local(): pl.pallas_call(body, out_shape=jax.ShapeDtypeStruct((owned, 3, half, poin...]
    ppermute x10 -> x0, waiting for transfers between devices: 37.4 us -> none  [the longest x4 28.2 us: padded(): before = lax.ppermute(last, axis, up)]
    ppermute x10 -> x0, starting transfers between devices: 30 us -> none  [the longest x4 15.9 us: padded(): before = lax.ppermute(last, axis, up)]
    concatenate x2 -> x0, other arithmetic: 6.06 us -> none  [padded(): shard = jnp.concatenate([before, shard, after], axis=dim)]
    unnamed x1 -> x0, blocking collectives: 5.41 us -> none
    slice x4 -> x0, other arithmetic: 5.31 us -> none  [padded(): last = lax.slice_in_dim(shard, length - width, length, axis=dim)]
    unnamed x42 -> x13, local copies, waits for them, and re-layouts: 1.93 us -> 6.97 us
  transfers between devices with their start and end apart: 10 -> 0, of which waited for: 7 -> 0; matrix products, arithmetic and copies ran while one was open for 4% -> 0% of each run, Pallas kernels for 0% -> 0%
where the time goes in v1:
time: 59.8 us; the launch traced here: 59.5 us
  Pallas kernels  52.5 us (88%)
  local copies, waits for them, and re-layouts  6.97 us (12%)
    pallas_call x1, Pallas kernels, local(): pl.pallas_call(body, out_shape=jax.ShapeDtypeStruct((owned, 3, half, poin...  52.5 us
    unnamed x13, local copies, waits for them, and re-layouts  6.97 us

profile of v1, /device:TPU:1, one launch (start us, length us, event | category | flops | bytes accessed | tf_op | source)
XLA Modules:
  0.0 59.5 jit_solution(7079489943741718444)
XLA Ops:
  0.0 0.0 copy-start
  0.0 1.5 %copy-done = f32[3,10,40,320]{3,2,1,0:T(8,128)S(1)} copy-done((f32[3,10,40,320]{3,2,1,0:T(8,128)S(1)}, f32[3,10,40,320]{3,2,1,0:T(8,128)}, u32[]{:S(2)}) %copy-start) | copy-done | bytes 1536024
  1.5 0.0 copy-start.1
  1.5 1.1 %copy-done.1 = f32[10,40,320]{2,1,0:T(8,128)S(1)} copy-done((f32[10,40,320]{2,1,0:T(8,128)S(1)}, f32[10,40,320]{2,1,0:T(8,128)}, u32[]{:S(2)}) %copy-start.1) | copy-done | bytes 512024
  2.6 0.0 copy-start.2
  2.6 1.1 %copy-done.2 = f32[10,40,320]{2,1,0:T(8,128)S(1)} copy-done((f32[10,40,320]{2,1,0:T(8,128)S(1)}, f32[10,40,320]{2,1,0:T(8,128)}, u32[]{:S(2)}) %copy-start.2) | copy-done | bytes 512024
  3.7 0.0 copy-start.3
  3.7 0.9 %copy-done.3 = bf16[2,2,80,200]{3,2,1,0:T(8,128)(2,1)S(1)} copy-done((bf16[2,2,80,200]{3,2,1,0:T(8,128)(2,1)S(1)}, bf16[2,2,80,200]{3,2,1,0:T(8,128)(2,1)}, u32[]{:S(2)}) %copy-start.3) | copy-done | bytes 128024
  4.6 0.0 copy-start.4
  4.6 0.9 %copy-done.4 = bf16[2,320,64]{2,1,0:T(8,128)(2,1)S(1)} copy-done((bf16[2,320,64]{2,1,0:T(8,128)(2,1)S(1)}, bf16[2,320,64]{2,1,0:T(8,128)(2,1)}, u32[]{:S(2)}) %copy-start.4) | copy-done | bytes 81944
  5.5 0.0 copy-start.5
  5.5 0.9 %copy-done.5 = f32[160,5]{1,0:T(8,128)S(1)} copy-done((f32[160,5]{1,0:T(8,128)S(1)}, f32[160,5]{1,0:T(8,128)}, u32[]{:S(2)}) %copy-start.5) | copy-done | bytes 3224
  6.4 52.5 %shard_map.64 = f32[2,3,8,64]{3,2,1,0:T(8,128)S(1)} custom-call(f32[160,5]{1,0:T(8,128)S(1)} %copy-done.5, f32[10,40,320]{2,1,0:T(8,128)S(1)} %copy-done.1, f32[10,40,320]{2,1,0:T(8,128)S(1)} %copy-done.2, f32[3,10,40,320]{3,2,1,0:T(8,128)S(1)} %copy-done, bf16[2,320,64]{2,1,0:T(8,128)(2,1)S(1)} %copy-done.4, bf16[2,2,80,200]{3,2,1,0:T(8,128)(2,1)S(1)} %copy-done.3), custom_call_target="tpu_custom_call" | custom-call | tf_op jit(solution)/shard_map/pallas_call | solution.py:363
  58.9 0.6 %copy.8 = f32[2,3,8,64]{3,2,1,0:T(8,128)} copy(f32[2,3,8,64]{3,2,1,0:T(8,128)S(1)} %shard_map.64) | data formatting | bytes 24576
Async XLA Ops:
  0.0 1.5 %copy-start = (f32[3,10,40,320]{3,2,1,0:T(8,128)S(1)}, f32[3,10,40,320]{3,2,1,0:T(8,128)}, u32[]{:S(2)}) copy-start(f32[3,10,40,320]{3,2,1,0:T(8,128)} %grad_ref.1) | copy-start | bytes 4608004
  1.5 1.1 %copy-start.1 = (f32[10,40,320]{2,1,0:T(8,128)S(1)}, f32[10,40,320]{2,1,0:T(8,128)}, u32[]{:S(2)}) copy-start(f32[10,40,320]{2,1,0:T(8,128)} %fixed_ref.1) | copy-start | bytes 1536004
  2.6 1.1 %copy-start.2 = (f32[10,40,320]{2,1,0:T(8,128)S(1)}, f32[10,40,320]{2,1,0:T(8,128)}, u32[]{:S(2)}) copy-start(f32[10,40,320]{2,1,0:T(8,128)} %moving_ref.1) | copy-start | bytes 1536004
  3.7 0.9 %copy-start.3 = (bf16[2,2,80,200]{3,2,1,0:T(8,128)(2,1)S(1)}, bf16[2,2,80,200]{3,2,1,0:T(8,128)(2,1)}, u32[]{:S(2)}) copy-start(bf16[2,2,80,200]{3,2,1,0:T(8,128)(2,1)} %constant.8.clone.by_ref) | copy-start | bytes 384004
  4.6 0.9 %copy-start.4 = (bf16[2,320,64]{2,1,0:T(8,128)(2,1)S(1)}, bf16[2,320,64]{2,1,0:T(8,128)(2,1)}, u32[]{:S(2)}) copy-start(bf16[2,320,64]{2,1,0:T(8,128)(2,1)} %constant.7.clone.bx_ref) | copy-start | bytes 245764
  5.5 0.9 %copy-start.5 = (f32[160,5]{1,0:T(8,128)S(1)}, f32[160,5]{1,0:T(8,128)}, u32[]{:S(2)}) copy-start(f32[160,5]{1,0:T(8,128)} %constant.6.clone.bz_ref) | copy-start | bytes 9604

commit v2 on v1

--- a/solution.py
+++ b/solution.py
@@ -17,16 +17,21 @@
 MESH = pl.DeviceIdType.MESH
 
 
+def spline_weights(u):
+    v = 1.0 - u
+    return [
+        v * v * v * (1.0 / 6.0),
+        (3.0 * u * u * u - 6.0 * u * u + 4.0) * (1.0 / 6.0),
+        (-3.0 * u * u * u + 3.0 * u * u + 3.0 * u + 1.0) * (1.0 / 6.0),
+        u * u * u * (1.0 / 6.0),
+    ]
+
+
 def spline_matrix(voxels, points):
     position = np.arange(voxels)
     cell = position // SPACING
     u = (position - cell * SPACING) / SPACING
-    weights = [
-        (1 - u) ** 3 / 6,
-        (3 * u**3 - 6 * u**2 + 4) / 6,
-        (-3 * u**3 + 3 * u**2 + 3 * u + 1) / 6,
-        u**3 / 6,
-    ]
+    weights = spline_weights(u)
     matrix = np.zeros((voxels, points))
     for k in range(4):
         np.add.at(matrix, (position, np.clip(cell - 1 + k, 0, points - 1)), weights[k])
@@ -56,8 +61,8 @@
 
 def kernel(
     gz_count, planes, height, width, points_y, points_x,
-    bz_ref, fixed_ref, moving_ref, grad_ref, bx_ref, by_ref, out_ref,
-    ext, grad, sums, boxes, coef, ksum, slope, acc, part, arrived,
+    fixed_ref, moving_ref, grad_ref, bx_hbm, by_hbm, band_hbm, out_ref,
+    bx_ref, by_ref, band, ext, grad, sums, boxes, coef, ksum, slope, acc, part, arrived,
     local_sem, z_send, z_recv, y_send, y_recv, p_send, p_recv,
 ):
     z, g = lax.axis_index("gz"), lax.axis_index("gy")
@@ -83,6 +88,11 @@
         )
         for i in range(2)
     ] + [pltpu.make_async_copy(grad_ref, grad, local_sem.at[2])]
+    tables = [
+        pltpu.make_async_copy(band_hbm, band, local_sem.at[3]),
+        pltpu.make_async_copy(bx_hbm, bx_ref, local_sem.at[4]),
+        pltpu.make_async_copy(by_hbm.at[g], by_ref, local_sem.at[5]),
+    ]
 
     ext[:, :, rows - 8 :, :] = jnp.zeros((2, ext.shape[1], 8, width), jnp.float32)
 
@@ -145,10 +155,12 @@
             for s in range(HALO):
                 for i in range(2):
                     z_copy(i, d, s).start()
-    local[2].start()
+    for copy in (tables[0], local[2], tables[1], tables[2]):
+        copy.start()
     for i in range(2):
         local[i].wait()
         y_own(i).wait_recv()
+    tables[0].wait()
 
     def relay(s):
         for d in range(2):
@@ -176,13 +188,26 @@
     lane = lax.broadcasted_iota(jnp.int32, (rows, lanes), 1)
     inside = (row >= RADIUS) & (row < rows - RADIUS) & (lane >= RADIUS) & (lane < width + RADIUS)
 
+    def band_dots(v, at, mid, end):
+        pieces = []
+        for _ in range(3):
+            piece = v.astype(jnp.bfloat16)
+            v = v - piece.astype(jnp.float32)
+            pieces.append(piece)
+        left = sum(dot(p[:, 0:256], band[:, at:mid]) for p in pieces)
+        right = sum(dot(p[:, 128:384], band[:, mid:end]) for p in pieces)
+        return left, right
+
     def coefficients(way, k):
-        for i in range(5):
-            boxes[i] = window_sum(window_sum(sums[way, i], 0, False), 1, False)
-        sf, sm = boxes[0], boxes[1]
-        cov = boxes[4] - sf * sm * (1.0 / WINDOW)
-        var_f = boxes[2] - sf * sf * (1.0 / WINDOW) + EPS
-        var_m = boxes[3] - sm * sm * (1.0 / WINDOW) + EPS
+        left, right = band_dots(sums[way].reshape(5 * rows, lanes), 0, 256, 384)
+        boxes[0 : 5 * rows, 0:256] = left
+        boxes[0 : 5 * rows, 256:] = right
+        sf, sm, sff, smm, sfm = (
+            window_sum(boxes[i * rows : (i + 1) * rows], 0, False) for i in range(5)
+        )
+        cov = sfm - sf * sm * (1.0 / WINDOW)
+        var_f = sff - sf * sf * (1.0 / WINDOW) + EPS
+        var_m = smm - sm * sm * (1.0 / WINDOW) + EPS
         at = z * planes + k - RADIUS
         valid = (at >= 0) & (at < gz_count * planes)
         keep = jnp.where(valid, 1.0, 0.0)
@@ -239,26 +264,31 @@
     for cell in range(owned):
         @pl.loop(cell * SPACING, (cell + 1) * SPACING)
         def _(o):
-            boxed = []
-            for i in range(3):
-                total = ksum[i] + coef[i, o + HALO]
-                ksum[i] = total - coef[i, o]
-                boxed.append(window_sum(window_sum(total, 0, True), 1, True))
+            total = ksum[...] + coef[:, o + HALO]
+            ksum[...] = total - coef[:, o]
+            left, right = band_dots(total.reshape(3 * rows, lanes), 384, 512, 768)
+            boxes[0 : 3 * rows, 0:128] = left
+            boxes[0 : 3 * rows, 128:] = right
+            boxed = [window_sum(boxes[i * rows : (i + 1) * rows], 0, True) for i in range(3)]
             slope[...] = (-2.0 * SIM_WEIGHT) * (
                 plane(0, o + HALO) * boxed[0] - plane(1, o + HALO) * boxed[1] - boxed[2]
             )
+            u = (o - cell * SPACING).astype(jnp.float32) * (1.0 / SPACING)
+            weights = spline_weights(u)
             own = slope[pl.ds(y0, height), 0:width]
             for c in range(3):
                 v = own * grad[c, o]
-                for j in range(cell, cell + 4):
-                    acc[c * cols + j] += bz_ref[z * planes + o, j] * v
-
+                for k in range(4):
+                    acc[c * cols + cell + k] += weights[k] * v
+
+    tables[1].wait()
+    tables[2].wait()
     for c in range(3):
         v = acc[c * cols : (c + 1) * cols].reshape(cols * height, width)
         hi, lo = split(v)
         along_x = dot(hi, bx_ref[0]) + dot(hi, bx_ref[1]) + dot(lo, bx_ref[0])
         hi, lo = split(along_x)
-        by_hi, by_lo = by_ref[g, 0], by_ref[g, 1]
+        by_hi, by_lo = by_ref[0], by_ref[1]
         along_y = dot(by_hi, hi) + dot(by_lo, hi) + dot(by_hi, lo)
         half = points_y // 2
         for j in range(cols):
@@ -266,6 +296,14 @@
                 at = j * points_y + h * half
                 part[h, j, c] = along_y[at : at + half]
 
+    @pl.when(jnp.logical_not(down))
+    def _():
+        part[:, 1] += part[:, 0]
+
+    @pl.when(jnp.logical_not(up))
+    def _():
+        part[:, owned] += part[:, owned + 1] + part[:, owned + 2]
+
     def p_copy(slot, half, first_row, count, dz, gy):
         return pltpu.make_async_remote_copy(
             part.at[half, pl.ds(first_row, count)],
@@ -337,10 +375,17 @@
     return np.stack([hi, lo])
 
 
+def band_matrices():
+    a, j = np.arange(256)[:, None], np.arange(384)[None, :]
+    back = np.concatenate([(j - a)[:, :256], (j - a - 128)[:, 256:]], axis=1)
+    ahead = np.concatenate([(a - j)[:, :128], (a + 128 - j)[:, 128:]], axis=1)
+    shift = np.concatenate([back, ahead], axis=1)
+    return ((shift >= 0) & (shift <= 2 * RADIUS)).astype(jnp.bfloat16)
+
+
 def local(gz_count, gy_count, fixed_image, moving_image, moving_grad):
     planes, height, width = fixed_image.shape
     points_x, points_y = width // SPACING, gy_count * height // SPACING
-    depth = gz_count * planes
     owned = planes // SPACING
     cols = owned + 3
     assert gy_count == 2 and planes >= HALO + 1 and owned >= 2 and height % 8 == 0
@@ -349,34 +394,35 @@
     by = np.stack(
         [hi_lo(np.kron(np.eye(cols), by_all[h * height : (h + 1) * height].T)) for h in range(2)]
     )
-    bz_all = np.pad(spline_matrix(depth, depth // SPACING), ((0, 0), (1, 2)))
-    bz = np.stack(
-        [bz_all[p, (p // planes) * owned : (p // planes) * owned + cols] for p in range(depth)]
-    ).astype(np.float32)
     rows = height + 2 * HALO
     lanes = (width + HALO + 127) // 128 * 128
     ext_planes = planes + 2 * HALO
+    assert lanes == 384
+    band = band_matrices()
     f32 = jnp.float32
     body = functools.partial(kernel, gz_count, planes, height, width, points_y, points_x)
-    vmem, smem, anyw = (pl.BlockSpec(memory_space=m) for m in (pltpu.VMEM, pltpu.SMEM, pl.ANY))
+    vmem, hbm = (pl.BlockSpec(memory_space=m) for m in (pltpu.VMEM, pltpu.HBM))
     half = points_y // 2
     return pl.pallas_call(
         body,
         out_shape=jax.ShapeDtypeStruct((owned, 3, half, points_x), f32),
-        in_specs=[smem, anyw, anyw, anyw, vmem, vmem],
+        in_specs=[hbm] * 6,
         out_specs=vmem,
         scratch_shapes=[
+            pltpu.VMEM(bx.shape, jnp.bfloat16),
+            pltpu.VMEM(by.shape[1:], jnp.bfloat16),
+            pltpu.VMEM(band.shape, jnp.bfloat16),
             pltpu.VMEM((2, ext_planes, rows, width), f32),
             pltpu.VMEM(moving_grad.shape, f32),
             pltpu.VMEM((2, 5, rows, lanes), f32),
-            pltpu.VMEM((5, rows, lanes), f32),
+            pltpu.VMEM((5 * rows, lanes), f32),
             pltpu.VMEM((3, planes + HALO, rows, lanes), f32),
             pltpu.VMEM((3, rows, lanes), f32),
             pltpu.VMEM((rows, lanes), f32),
             pltpu.VMEM((3 * cols, height, width), f32),
             pltpu.VMEM((2, cols, 3, half, points_x), f32),
             pltpu.VMEM((5, owned, 3, half, points_x), f32),
-            pltpu.SemaphoreType.DMA((3,)),
+            pltpu.SemaphoreType.DMA((6,)),
             pltpu.SemaphoreType.DMA((2, 2, HALO)),
             pltpu.SemaphoreType.DMA((2, 2, HALO)),
             pltpu.SemaphoreType.DMA((3, HALO)),
@@ -387,7 +433,7 @@
         compiler_params=pltpu.CompilerParams(
             collective_id=0, has_side_effects=True, vmem_limit_bytes=40 * 2**20
         ),
-    )(jnp.asarray(bz), fixed_image, moving_image, moving_grad, jnp.asarray(bx), jnp.asarray(by))
+    )(fixed_image, moving_image, moving_grad, jnp.asarray(bx), jnp.asarray(by), jnp.asarray(band))
 
 
 def solution(mesh):

time: 59.8 us -> 52.4 us (0.88)
  Pallas kernels: 52.5 us -> 45 us
    pallas_call x1, Pallas kernels: 52.5 us -> 45 us  [local(): pl.pallas_call(body, out_shape=jax.ShapeDtypeStruct((owned, 3, half, poin...]
where the time goes in v2:
time: 52.4 us; the launch traced here: 52.1 us
  Pallas kernels  45 us (86%)
  local copies, waits for them, and re-layouts  7.08 us (14%)
    pallas_call x1, Pallas kernels, local(): pl.pallas_call(body, out_shape=jax.ShapeDtypeStruct((owned, 3, half, poin...  45 us
    unnamed x13, local copies, waits for them, and re-layouts  7.08 us

profile of v2, /device:TPU:1, one launch (start us, length us, event | category | flops | bytes accessed | tf_op | source)
XLA Modules:
  0.0 52.1 jit_solution(14952718128610475123)
XLA Ops:
  0.0 0.0 copy-start
  0.0 1.5 %copy-done = f32[3,10,40,320]{3,2,1,0:T(8,128)S(1)} copy-done((f32[3,10,40,320]{3,2,1,0:T(8,128)S(1)}, f32[3,10,40,320]{3,2,1,0:T(8,128)}, u32[]{:S(2)}) %copy-start) | copy-done | bytes 1536024
  1.5 0.0 copy-start.1
  1.5 1.1 %copy-done.1 = f32[10,40,320]{2,1,0:T(8,128)S(1)} copy-done((f32[10,40,320]{2,1,0:T(8,128)S(1)}, f32[10,40,320]{2,1,0:T(8,128)}, u32[]{:S(2)}) %copy-start.1) | copy-done | bytes 512024
  2.6 0.0 copy-start.2
  2.6 1.1 %copy-done.2 = f32[10,40,320]{2,1,0:T(8,128)S(1)} copy-done((f32[10,40,320]{2,1,0:T(8,128)S(1)}, f32[10,40,320]{2,1,0:T(8,128)}, u32[]{:S(2)}) %copy-start.2) | copy-done | bytes 512024
  3.7 0.0 copy-start.3
  3.7 1.0 %copy-done.3 = bf16[256,768]{1,0:T(8,128)(2,1)S(1)} copy-done((bf16[256,768]{1,0:T(8,128)(2,1)S(1)}, bf16[256,768]{1,0:T(8,128)(2,1)}, u32[]{:S(2)}) %copy-start.3) | copy-done | bytes 393240
  4.6 0.0 copy-start.4
  4.6 0.9 %copy-done.4 = bf16[2,2,80,200]{3,2,1,0:T(8,128)(2,1)S(1)} copy-done((bf16[2,2,80,200]{3,2,1,0:T(8,128)(2,1)S(1)}, bf16[2,2,80,200]{3,2,1,0:T(8,128)(2,1)}, u32[]{:S(2)}) %copy-start.4) | copy-done | bytes 128024
  5.6 0.0 copy-start.5
  5.6 0.9 %copy-done.5 = bf16[2,320,64]{2,1,0:T(8,128)(2,1)S(1)} copy-done((bf16[2,320,64]{2,1,0:T(8,128)(2,1)S(1)}, bf16[2,320,64]{2,1,0:T(8,128)(2,1)}, u32[]{:S(2)}) %copy-start.5) | copy-done | bytes 81944
  6.5 45.0 %shard_map.64 = f32[2,3,8,64]{3,2,1,0:T(8,128)S(1)} custom-call(f32[10,40,320]{2,1,0:T(8,128)S(1)} %copy-done.1, f32[10,40,320]{2,1,0:T(8,128)S(1)} %copy-done.2, f32[3,10,40,320]{3,2,1,0:T(8,128)S(1)} %copy-done, bf16[2,320,64]{2,1,0:T(8,128)(2,1)S(1)} %copy-done.5, bf16[2,2,80,200]{3,2,1,0:T(8,128)(2,1)S(1)} %copy-done.4, bf16[256,768]{1,0:T(8,128)(2,1)S(1)} %copy-done.3), custom_call_target="tpu_custom_call" | custom-call | tf_op jit(solution)/shard_map/pallas_call | solution.py:406
  51.5 0.6 %copy.8 = f32[2,3,8,64]{3,2,1,0:T(8,128)} copy(f32[2,3,8,64]{3,2,1,0:T(8,128)S(1)} %shard_map.64) | data formatting | bytes 24576
Async XLA Ops:
  0.0 1.5 %copy-start = (f32[3,10,40,320]{3,2,1,0:T(8,128)S(1)}, f32[3,10,40,320]{3,2,1,0:T(8,128)}, u32[]{:S(2)}) copy-start(f32[3,10,40,320]{3,2,1,0:T(8,128)} %grad_ref.1) | copy-start | bytes 4608004
  1.5 1.1 %copy-start.1 = (f32[10,40,320]{2,1,0:T(8,128)S(1)}, f32[10,40,320]{2,1,0:T(8,128)}, u32[]{:S(2)}) copy-start(f32[10,40,320]{2,1,0:T(8,128)} %fixed_ref.1) | copy-start | bytes 1536004
  2.6 1.1 %copy-start.2 = (f32[10,40,320]{2,1,0:T(8,128)S(1)}, f32[10,40,320]{2,1,0:T(8,128)}, u32[]{:S(2)}) copy-start(f32[10,40,320]{2,1,0:T(8,128)} %moving_ref.1) | copy-start | bytes 1536004
  3.7 1.0 %copy-start.3 = (bf16[256,768]{1,0:T(8,128)(2,1)S(1)}, bf16[256,768]{1,0:T(8,128)(2,1)}, u32[]{:S(2)}) copy-start(bf16[256,768]{1,0:T(8,128)(2,1)} %constant.8.clone.band_hbm) | copy-start | bytes 1179652
  4.6 0.9 %copy-start.4 = (bf16[2,2,80,200]{3,2,1,0:T(8,128)(2,1)S(1)}, bf16[2,2,80,200]{3,2,1,0:T(8,128)(2,1)}, u32[]{:S(2)}) copy-start(bf16[2,2,80,200]{3,2,1,0:T(8,128)(2,1)} %constant.7.clone.by_hbm) | copy-start | bytes 384004
  5.6 0.9 %copy-start.5 = (bf16[2,320,64]{2,1,0:T(8,128)(2,1)S(1)}, bf16[2,320,64]{2,1,0:T(8,128)(2,1)}, u32[]{:S(2)}) copy-start(bf16[2,320,64]{2,1,0:T(8,128)(2,1)} %constant.6.clone.bx_hbm) | copy-start | bytes 245764

commit v3 on v2

--- a/solution.py
+++ b/solution.py
@@ -62,7 +62,7 @@
 def kernel(
     gz_count, planes, height, width, points_y, points_x,
     fixed_ref, moving_ref, grad_ref, bx_hbm, by_hbm, band_hbm, out_ref,
-    bx_ref, by_ref, band, ext, grad, sums, boxes, coef, ksum, slope, acc, part, arrived,
+    bx_ref, by_ref, band, raw, ext, grad, sums, boxes, coef, ksum, slope, acc, part, arrived,
     local_sem, z_send, z_recv, y_send, y_recv, p_send, p_recv,
 ):
     z, g = lax.axis_index("gz"), lax.axis_index("gy")
@@ -72,37 +72,31 @@
     y0 = pl.multiple_of(g * HALO, 8)
     y_src = pl.multiple_of(jnp.where(g == 0, height - HALO, HALO), 8)
     y_dst = pl.multiple_of(jnp.where(g == 0, 0, height), 8)
-    own_src = pl.multiple_of(jnp.where(g == 0, height - HALO, 0), 8)
     owned = planes // SPACING
     cols = owned + 3
     images = (fixed_ref, moving_ref)
 
-    def window(p, i):
-        return ext.at[i, p, pl.ds(y0, height)]
-
-    local = [
-        pltpu.make_async_copy(
-            images[i],
-            ext.at[i, pl.ds(HALO, planes), pl.ds(y0, height)],
-            local_sem.at[i],
-        )
-        for i in range(2)
-    ] + [pltpu.make_async_copy(grad_ref, grad, local_sem.at[2])]
+    local = [pltpu.make_async_copy(images[i], raw.at[i], local_sem.at[i]) for i in range(2)]
+    local.append(pltpu.make_async_copy(grad_ref, grad, local_sem.at[2]))
     tables = [
         pltpu.make_async_copy(band_hbm, band, local_sem.at[3]),
         pltpu.make_async_copy(bx_hbm, bx_ref, local_sem.at[4]),
         pltpu.make_async_copy(by_hbm.at[g], by_ref, local_sem.at[5]),
     ]
 
-    ext[:, :, rows - 8 :, :] = jnp.zeros((2, ext.shape[1], 8, width), jnp.float32)
+    for copy in (*local, *tables):
+        copy.start()
+
+    ext_planes, packed = ext.shape[0], ext.shape[2]
+    ext[:, rows - 8 :, :] = jnp.zeros((ext_planes, 8, packed), jnp.float32)
 
     @pl.when(jnp.logical_not(down))
     def _():
-        ext[:, 0:HALO] = jnp.zeros((2, HALO, rows, width), jnp.float32)
+        ext[0:HALO] = jnp.zeros((HALO, rows, packed), jnp.float32)
 
     @pl.when(jnp.logical_not(up))
     def _():
-        ext[:, HALO + planes :] = jnp.zeros((2, HALO, rows, width), jnp.float32)
+        ext[HALO + planes :] = jnp.zeros((HALO, rows, packed), jnp.float32)
 
     barrier = pltpu.get_barrier_semaphore()
 
@@ -115,59 +109,59 @@
     for gy in (g, other):
         greet(up, 1, gy)
         greet(down, -1, gy)
+    for i in range(2):
+        local[i].wait()
+    tail = width - 256
+
+    @pl.loop(0, planes)
+    def _(p):
+        at = (HALO + p, pl.ds(y0, height))
+        ext[(*at, slice(0, 256))] = raw[0, p, :, 0:256]
+        ext[(*at, slice(256, 512))] = raw[1, p, :, 0:256]
+        ext[(*at, slice(512, 640))] = jnp.concatenate(
+            [raw[0, p, :, 256:width], raw[1, p, :, 256:width]], axis=1
+        )
+
     pl.semaphore_wait(barrier, 1 + 2 * up.astype(jnp.int32) + 2 * down.astype(jnp.int32))
 
-    def z_copy(i, d, s):
-        src = planes - 1 - s if d == 0 else s
+    def z_copy(d, s):
+        src = HALO + planes - 1 - s if d == 0 else HALO + s
         dst = HALO - 1 - s if d == 0 else HALO + planes + s
         return pltpu.make_async_remote_copy(
-            images[i].at[src], window(dst, i),
-            z_send.at[i, d, s], z_recv.at[i, d, s],
+            ext.at[src, pl.ds(y0, height)], ext.at[dst, pl.ds(y0, height)],
+            z_send.at[d, s], z_recv.at[d, s],
             device_id={"gz": z + 1 if d == 0 else z - 1, "gy": g}, device_id_type=MESH,
         )
 
-    def y_own(i):
+    def y_copy(at, d, s):
         return pltpu.make_async_remote_copy(
-            images[i].at[:, pl.ds(own_src, HALO), :],
-            ext.at[i, pl.ds(HALO, planes), pl.ds(y_dst, HALO)],
-            y_send.at[2, i], y_recv.at[2, i],
-            device_id={"gz": z, "gy": other}, device_id_type=MESH,
-        )
-
-    def y_relay(d, s):
-        p = HALO - 1 - s if d == 0 else HALO + planes + s
-        return pltpu.make_async_remote_copy(
-            ext.at[:, p, pl.ds(y_src, HALO)],
-            ext.at[:, p, pl.ds(y_dst, HALO)],
+            ext.at[at, pl.ds(y_src, HALO)], ext.at[at, pl.ds(y_dst, HALO)],
             y_send.at[d, s], y_recv.at[d, s],
             device_id={"gz": z, "gy": other}, device_id_type=MESH,
         )
 
+    y_own = y_copy(pl.ds(HALO, planes), 2, 0)
+
+    def y_relay(d, s):
+        return y_copy(HALO - 1 - s if d == 0 else HALO + planes + s, d, s)
+
     sends = (up, down)
     takes = (down, up)
 
-    for i in range(2):
-        local[i].start()
-        y_own(i).start()
-    for d in range(2):
-        @pl.when(sends[d])
-        def _():
-            for s in range(HALO):
-                for i in range(2):
-                    z_copy(i, d, s).start()
-    for copy in (tables[0], local[2], tables[1], tables[2]):
-        copy.start()
-    for i in range(2):
-        local[i].wait()
-        y_own(i).wait_recv()
+    y_own.start()
+    for s in range(HALO):
+        for d in range(2):
+            @pl.when(sends[d])
+            def _():
+                z_copy(d, s).start()
+    y_own.wait_recv()
     tables[0].wait()
 
     def relay(s):
         for d in range(2):
             @pl.when(takes[d])
             def _():
-                for i in range(2):
-                    z_copy(i, d, s).wait_recv()
+                z_copy(d, s).wait_recv()
                 y_relay(d, s).start()
 
     def ready(d, s):
@@ -175,10 +169,14 @@
         def _():
             y_relay(d, s).wait_recv()
 
-    pad = jnp.zeros((rows, lanes - width), jnp.float32)
+    in_tail = lax.broadcasted_iota(jnp.int32, (rows, 128), 1) < tail
 
     def plane(i, p):
-        return jnp.concatenate([ext[i, p], pad], axis=1)
+        last = ext[p, :, 512:640]
+        if i == 1:
+            last = pltpu.roll(last, 128 - tail, 1)
+        last = jnp.where(in_tail, last, 0.0)
+        return jnp.concatenate([ext[p, :, 256 * i : 256 * (i + 1)], last], axis=1)
 
     def fields(p):
         f, m = plane(0, p), plane(1, p)
@@ -238,6 +236,28 @@
     for j in range(first):
         move(0, 2 * HALO + 1 + j, HALO + j, HALO + 1 + j)
 
+    acc[...] = jnp.zeros(acc.shape, jnp.float32)
+    local[2].wait()
+
+    def output(way, o, new, old):
+        total = ksum[way] + coef[:, new] - coef[:, old]
+        ksum[way] = total
+        left, right = band_dots(total.reshape(3 * rows, lanes), 384, 512, 768)
+        boxes[0 : 3 * rows, 0:128] = left
+        boxes[0 : 3 * rows, 128:] = right
+        boxed = [window_sum(boxes[i * rows : (i + 1) * rows], 0, True) for i in range(3)]
+        slope[...] = (-2.0 * SIM_WEIGHT) * (
+            plane(0, o + HALO) * boxed[0] - plane(1, o + HALO) * boxed[1] - boxed[2]
+        )
+        cell = lax.div(o, SPACING)
+        weights = spline_weights((o - cell * SPACING).astype(jnp.float32) * (1.0 / SPACING))
+        own = slope[pl.ds(y0, height), 0:width]
+        for c in range(3):
+            v = own * grad[c, o]
+            for k in range(4):
+                acc[c * cols + cell + k] += weights[k] * v
+
+    meet = HALO - planes // 2
     relay(0)
 
     @pl.loop(0, HALO)
@@ -251,35 +271,20 @@
         ready(1, s)
         move(0, HALO + planes + s, planes - 1 + s, planes + s)
 
-    for i in range(3):
-        ksum[i] = jnp.zeros((rows, lanes), jnp.float32)
-    acc[...] = jnp.zeros(acc.shape, jnp.float32)
-
-    @pl.loop(0, HALO)
-    def _(k):
-        for i in range(3):
-            ksum[i] += coef[i, k]
-
-    local[2].wait()
-    for cell in range(owned):
-        @pl.loop(cell * SPACING, (cell + 1) * SPACING)
-        def _(o):
-            total = ksum[...] + coef[:, o + HALO]
-            ksum[...] = total - coef[:, o]
-            left, right = band_dots(total.reshape(3 * rows, lanes), 384, 512, 768)
-            boxes[0 : 3 * rows, 0:128] = left
-            boxes[0 : 3 * rows, 128:] = right
-            boxed = [window_sum(boxes[i * rows : (i + 1) * rows], 0, True) for i in range(3)]
-            slope[...] = (-2.0 * SIM_WEIGHT) * (
-                plane(0, o + HALO) * boxed[0] - plane(1, o + HALO) * boxed[1] - boxed[2]
-            )
-            u = (o - cell * SPACING).astype(jnp.float32) * (1.0 / SPACING)
-            weights = spline_weights(u)
-            own = slope[pl.ds(y0, height), 0:width]
-            for c in range(3):
-                v = own * grad[c, o]
-                for k in range(4):
-                    acc[c * cols + cell + k] += weights[k] * v
+        @pl.when(s == meet)
+        def _():
+            for way, start in ((1, HALO - meet), (0, planes - HALO - 1 + meet)):
+                ksum[way] = coef[:, start]
+
+                @pl.loop(start + 1, start + HALO + 1)
+                def _(k):
+                    ksum[way] += coef[:, k]
+
+        @pl.when(s >= meet)
+        def _():
+            low, high = HALO - 1 - s, planes - HALO + s
+            output(1, low, low, low + HALO + 1)
+            output(0, high, high + HALO, high - 1)
 
     tables[1].wait()
     tables[2].wait()
@@ -343,8 +348,7 @@
         out_ref[owned - 1 : owned] += arrived[3, 0:1] + arrived[4, 0:1]
 
     partner.wait_send()
-    for i in range(2):
-        y_own(i).wait_send()
+    y_own.wait_send()
 
     @pl.when(up)
     def _():
@@ -360,8 +364,7 @@
         @pl.when(sends[d])
         def _():
             for s in range(HALO):
-                for i in range(2):
-                    z_copy(i, d, s).wait_send()
+                z_copy(d, s).wait_send()
 
         @pl.when(takes[d])
         def _():
@@ -397,7 +400,7 @@
     rows = height + 2 * HALO
     lanes = (width + HALO + 127) // 128 * 128
     ext_planes = planes + 2 * HALO
-    assert lanes == 384
+    assert lanes == 384 and 256 < width <= 320 and planes % 2 == 0 and planes <= 2 * HALO
     band = band_matrices()
     f32 = jnp.float32
     body = functools.partial(kernel, gz_count, planes, height, width, points_y, points_x)
@@ -412,26 +415,27 @@
             pltpu.VMEM(bx.shape, jnp.bfloat16),
             pltpu.VMEM(by.shape[1:], jnp.bfloat16),
             pltpu.VMEM(band.shape, jnp.bfloat16),
-            pltpu.VMEM((2, ext_planes, rows, width), f32),
+            pltpu.VMEM((2, planes, height, width), f32),
+            pltpu.VMEM((ext_planes, rows, 640), f32),
             pltpu.VMEM(moving_grad.shape, f32),
             pltpu.VMEM((2, 5, rows, lanes), f32),
             pltpu.VMEM((5 * rows, lanes), f32),
             pltpu.VMEM((3, planes + HALO, rows, lanes), f32),
-            pltpu.VMEM((3, rows, lanes), f32),
+            pltpu.VMEM((2, 3, rows, lanes), f32),
             pltpu.VMEM((rows, lanes), f32),
             pltpu.VMEM((3 * cols, height, width), f32),
             pltpu.VMEM((2, cols, 3, half, points_x), f32),
             pltpu.VMEM((5, owned, 3, half, points_x), f32),
             pltpu.SemaphoreType.DMA((6,)),
-            pltpu.SemaphoreType.DMA((2, 2, HALO)),
-            pltpu.SemaphoreType.DMA((2, 2, HALO)),
+            pltpu.SemaphoreType.DMA((2, HALO)),
+            pltpu.SemaphoreType.DMA((2, HALO)),
             pltpu.SemaphoreType.DMA((3, HALO)),
             pltpu.SemaphoreType.DMA((3, HALO)),
             pltpu.SemaphoreType.DMA((5,)),
             pltpu.SemaphoreType.DMA((5,)),
         ],
         compiler_params=pltpu.CompilerParams(
-            collective_id=0, has_side_effects=True, vmem_limit_bytes=40 * 2**20
+            collective_id=0, has_side_effects=True, vmem_limit_bytes=60 * 2**20
         ),
     )(fixed_image, moving_image, moving_grad, jnp.asarray(bx), jnp.asarray(by), jnp.asarray(band))
 

time: 52.4 us -> 42.1 us (0.80)
  local copies, waits for them, and re-layouts: 7.08 us -> 1.35 us
  Pallas kernels: 45 us -> 40.6 us
    unnamed x13 -> x1, local copies, waits for them, and re-layouts: 7.08 us -> 1.35 us
    pallas_call x1, Pallas kernels: 45 us -> 40.6 us  [local(): pl.pallas_call(body, out_shape=jax.ShapeDtypeStruct((owned, 3, half, poin...]
where the time goes in v3:
time: 42.1 us; the launch traced here: 42 us
  Pallas kernels  40.6 us (96%)
  local copies, waits for them, and re-layouts  1.35 us (3%)
    pallas_call x1, Pallas kernels, local(): pl.pallas_call(body, out_shape=jax.ShapeDtypeStruct((owned, 3, half, poin...  40.6 us
    unnamed x1, local copies, waits for them, and re-layouts  1.35 us

profile of v3, /device:TPU:1, one launch (start us, length us, event | category | flops | bytes accessed | tf_op | source)
XLA Modules:
  0.0 42.0 jit_solution(12723513856492633157)
XLA Ops:
  0.0 40.6 %shard_map.64 = f32[2,3,8,64]{3,2,1,0:T(8,128)} custom-call(f32[10,40,320]{2,1,0:T(8,128)} %fixed_ref.1, f32[10,40,320]{2,1,0:T(8,128)} %moving_ref.1, f32[3,10,40,320]{3,2,1,0:T(8,128)} %grad_ref.1, bf16[2,320,64]{2,1,0:T(8,128)(2,1)} %constant.6.clone.bx_hbm, bf16[2,2,80,200]{3,2,1,0:T(8,128)(2,1)} %constant.7.clone.by_hbm, ...), custom_call_target="tpu_custom_call" | custom-call | tf_op jit(solution)/shard_map/pallas_call | solution.py:409
  40.6 1.3 %copy.8 = f32[2,3,8,64]{3,2,1,0:T(8,128)} copy(f32[2,3,8,64]{3,2,1,0:T(8,128)} %shard_map.64) | data formatting | bytes 24576
